TPU v7x, 32 devices: a whole 2x2x4 slice. The times are simulated.
32 devices in a mesh: row: 2 (over y), col: 4 (over x, core), rep: 4 (over z).
Axes of the slice: x: 2, y: 2, z: 4, core: 2. Of those that a mesh axis runs over, the one named last changes fastest.
Arguments:
- hidden: bfloat16 [512, 7168], P('rep'), may hold values from -6 to 6
- train_weight: bfloat16 [7168, 16384], P(('rep', 'row'), 'col'), may hold values from -0.0625 to 0.0625
- shard_order: int32 [4, 4, 2], replicated, may hold values from 0 to 1, each once within a row
Outputs:
- served_weight: bfloat16 [7168, 16384], P(None, ('col', 'row'))
- projected: float32 [512, 16384], P('rep', ('col', 'row'))
Inputs may be any that keep to these rules, and one draw needn't show every extreme that they name: Each shard_order[c, k] is a permutation of 0 to 1.
All inputs are finite; a program needn't handle non-finite values.
Results may differ from a plain program's by a relative error of at most 0.001.
Values may be sent and summed in bfloat16 or wider, within the bound.
A program may use at most 128 MiB of HBM per device.

v0:
```python
import jax
import jax.numpy as jnp
from jax import lax
from jax.sharding import PartitionSpec as P


def shards(hidden, train_weight, shard_order):
    row_count = lax.axis_size("row")
    rows_tile = train_weight.shape[0]
    cols_tile = train_weight.shape[1]
    piece_cols = cols_tile // row_count
    sub_count = shard_order.shape[1]
    sub_cols = piece_cols // sub_count
    my_order = lax.dynamic_index_in_dim(shard_order, lax.axis_index("col"), 0, keepdims=False)
    source_ids = lax.broadcasted_iota(jnp.int32, (sub_count, row_count, row_count), 2)
    selector = (my_order[:, :, None] == source_ids).astype(jnp.bfloat16)
    tiled = train_weight.reshape(rows_tile, row_count, sub_count, sub_cols)
    picked = jnp.einsum("ksj,rjkc->rskc", selector, tiled, preferred_element_type=jnp.float32)
    ordered = picked.astype(jnp.bfloat16).reshape(rows_tile, cols_tile)
    column = lax.all_to_all(ordered, "row", split_axis=1, concat_axis=0, tiled=True)
    served = lax.all_gather(column, "rep", axis=0, tiled=True)
    projected = jnp.dot(hidden, served, preferred_element_type=jnp.float32)
    return (served, projected)


def solution(mesh):
    placed = (P("rep", None), P(("rep", "row"), "col"), P())
    return jax.shard_map(
        shards,
        mesh=mesh,
        in_specs=placed,
        out_specs=(P(None, ("col", "row")), P("rep", ("col", "row"))),
        check_vma=False,
    )
```

profile of v0, /device:TPU:0, one launch (start us, length us, event | category | flops | bytes accessed | tf_op | source)
XLA Modules:
  0.0 697.5 jit_solution(17215963833131791758)
XLA Ops:
  7.2 0.0 copy-start
  7.2 0.0 all-gather.2.cloned.1.call-start
  7.2 0.8 dynamic-slice_bitcast_fusion
  8.0 0.1 copy.12
  8.1 12.8 %reshape.14 = bf16[896,2,4,512]{3,2,1,0:T(4,128)(2,1)} reshape(bf16[896,4096]{1,0:T(8,128)(2,1)} %param.4) | data formatting | bytes 14680064 | tf_op jit(solution)/shard_map/reshape | solution.py:17
  21.0 18.4 %fusion = bf16[896,2,4,512]{3,1,0,2:T(2,128)(2,1)} fusion(bf16[896,2,4,512]{3,2,1,0:T(4,128)(2,1)} %reshape.14, s32[4,2]{1,0:T(4,128)S(1)} %copy.12), kind=kOutput, calls=%fused_computation.1 | convolution fusion | flops 18350096 | bytes 14680096 | tf_op jit(solution)/shard_map/ksj,rjkc->rskc/dot_general | solution.py:18
  39.3 18.6 %copy.14 = bf16[896,2,4,512]{0,3,2,1:T(8,128)(2,1)} copy(bf16[896,2,4,512]{3,1,0,2:T(2,128)(2,1)} %fusion) | data formatting | bytes 14680064 | tf_op jit(solution)/shard_map/convert_element_type | solution.py:19
  57.9 92.8 %all_to_all.19 = bf16[896,2,2048]{0,2,1:T(8,128)(2,1)} all-to-all(bf16[896,2,2048]{0,2,1:T(8,128)(2,1)} %bitcast.17), channel_id=1, replica_groups=mesh['row'=2,'col'=4,'rep'=4] {'row'}, dimensions={1} | all-to-all | bytes 14680064 | tf_op jit(solution)/shard_map/all_to_all | solution.py:20
  150.8 11.3 %copy.15 = bf16[2,896,2048]{2,1,0:T(8,128)(2,1)} copy(bf16[2,896,2048]{1,2,0:T(8,128)(2,1)} %bitcast.18) | data formatting | bytes 14680064 | tf_op jit(solution)/shard_map/all_to_all | solution.py:20
  162.0 0.0 all-gather.2.cloned.1.call-update
  162.1 493.7 %all-gather.2.cloned.1.call-done = bf16[7168,2048]{1,0:T(8,128)(2,1)} async-done(((bf16[1792,2048]{1,0:T(8,128)(2,1)}), bf16[7168,2048]{1,0:T(8,128)(2,1)}) %all-gather.2.cloned.1.call-update) | async-done | bytes 29360144 | tf_op jit(solution)/shard_map/all_gather | solution.py:21
  655.8 0.0 copy-done
  655.8 13.3 %convolution_bitcast_fusion = f32[128,2048]{0,1:T(8,128)S(1)} fusion(bf16[7168,2048]{1,0:T(8,128)(2,1)} %all-gather.2.cloned.1.call-done, bf16[128,7168]{1,0:T(8,128)(2,1)S(1)} %copy-done), kind=kOutput, calls=%fused_computation.3 | convolution fusion | flops 3758096384 | bytes 32243712 | tf_op jit(solution)/shard_map/dot_general | solution.py:22
  669.1 1.3 copy.16
  670.4 0.0 copy-start.1
  670.4 20.2 %copy.21 = bf16[7168,2048]{1,0:T(8,128)(2,1)} copy(bf16[7168,2048]{1,0:T(8,128)(2,1)} %all-gather.2.cloned.1.call-done) | data formatting | bytes 58720256
  690.6 0.0 copy-done.1
Async XLA Ops:
  7.2 648.6 %copy-start = (bf16[128,7168]{1,0:T(8,128)(2,1)S(1)}, bf16[128,7168]{1,0:T(8,128)(2,1)}, u32[]{:S(2)}) copy-start(bf16[128,7168]{1,0:T(8,128)(2,1)} %param.3) | copy-start | bytes 5505028
  7.2 648.6 %all-gather.2.cloned.1.call-start = ((), (), s32[]{:S(2)}) async-start(), calls=%async_computation.1 | async-start | bytes 36700160 | tf_op jit(solution)/shard_map/all_gather | solution.py:21
  670.4 20.2 %copy-start.1 = (bf16[128,7168]{1,0:T(8,128)(2,1)S(1)}, bf16[128,7168]{1,0:T(8,128)(2,1)}, u32[]{:S(2)}) copy-start(bf16[128,7168]{1,0:T(8,128)(2,1)} %param.3) | copy-start | bytes 5505028
Sparse Core Ops, SparseCore 0:
  162.2 493.5 all-gather.1
where the time goes:
time: 699 us; the launch traced here: 697 us
  waiting for transfers between devices  494 us (71%)
  blocking collectives  92.8 us (13%)
  local copies, waits for them, and re-layouts  65.1 us (9%)
  matrix products  31.7 us (5%)
  between operations  14.1 us (2%)
    all_gather x1, waiting for transfers between devices, shards(): served = lax.all_gather(column, 'rep', axis=0, tiled=True)  494 us
    all_to_all x1, blocking collectives, shards(): lax.all_to_all(ordered, 'row', split_axis=1, concat_axis=0, tiled=True)  92.8 us
    unnamed x6, local copies, waits for them, and re-layouts  21.5 us
    convert_element_type x1, local copies, waits for them, and re-layouts, shards(): ordered = picked.astype(jnp.bfloat16).reshape(rows_tile, cols_tile)  18.6 us
    dot_general x1, matrix products, shards(): jnp.einsum('ksj,rjkc->rskc', selector, tiled, preferred_element_type=jnp....  18.4 us
  transfers between devices with their start and end apart: 1, of which 1 were waited for; matrix products, arithmetic and copies ran while one was open for 0% of the time, Pallas kernels for 0%

commit v1 on v0

v1 whole, which is shorter than its diff:
```python
import functools

import jax
import jax.numpy as jnp
from jax import lax
from jax.experimental import pallas as pl
from jax.experimental.pallas import tpu as pltpu
from jax.sharding import PartitionSpec as P

MESH = pl.DeviceIdType.MESH
LANES = 128
VMEM_LIMIT = 8 * 1024 * 1024


def order_kernel(order_ref, tile_ref, out_ref, sem):
    _, sub_count, row_count = order_ref.shape
    c = lax.axis_index("col")
    piece_cols = out_ref.shape[2]
    sub_cols = piece_cols // sub_count
    copies = []
    for s in range(row_count):
        for k in range(sub_count):
            start = pl.multiple_of(order_ref[c, k, s] * piece_cols + k * sub_cols, LANES)
            copies.append(
                pltpu.make_async_copy(
                    tile_ref.at[:, pl.ds(start, sub_cols)],
                    out_ref.at[s, :, pl.ds(k * sub_cols, sub_cols)],
                    sem.at[s * sub_count + k],
                )
            )
    for copy in copies:
        copy.start()
    for copy in copies:
        copy.wait()


def ordered_pieces(tile, shard_order):
    _, sub_count, row_count = shard_order.shape
    rows_tile, cols_tile = tile.shape
    piece_cols = cols_tile // row_count
    sub_cols = piece_cols // sub_count
    if sub_cols % LANES == 0:
        return pl.pallas_call(
            order_kernel,
            out_shape=pltpu.VMEM((row_count, rows_tile, piece_cols), tile.dtype),
            in_specs=[
                pl.BlockSpec(memory_space=pltpu.SMEM),
                pl.BlockSpec(memory_space=pltpu.HBM),
            ],
            out_specs=pl.BlockSpec(memory_space=pltpu.VMEM),
            scratch_shapes=[pltpu.SemaphoreType.DMA((row_count * sub_count,))],
            compiler_params=pltpu.CompilerParams(vmem_limit_bytes=VMEM_LIMIT),
        )(shard_order, pltpu.with_memory_space_constraint(tile, pltpu.HBM))
    my_order = lax.dynamic_index_in_dim(shard_order, lax.axis_index("col"), 0, keepdims=False)
    blocks = tile.reshape(rows_tile, row_count, sub_count, sub_cols)
    pieces = []
    for s in range(row_count):
        piece = blocks[:, 0]
        for j in range(1, row_count):
            piece = jnp.where((my_order[:, s] == j)[None, :, None], blocks[:, j], piece)
        pieces.append(piece.reshape(rows_tile, piece_cols))
    return jnp.stack(pieces)


def gather_kernel(n_row, n_rep, chunks, own_ref, out_ref, y_send, y_recv, z_recv, up_send, down_send):
    r, c, z = lax.axis_index("row"), lax.axis_index("col"), lax.axis_index("rep")
    rows_tile = own_ref.shape[1]
    rows = rows_tile // chunks
    has_up, has_down = z < n_rep - 1, z > 0
    above = (r, c, jnp.minimum(z + 1, n_rep - 1))
    below = (r, c, jnp.maximum(z - 1, 0))
    per_level = n_row * chunks

    barrier = pltpu.get_barrier_semaphore()
    for t in range(1, n_row):
        pl.semaphore_signal(barrier, inc=1, device_id=(lax.rem(r + t, n_row), c, z), device_id_type=MESH)

    @pl.when(has_up)
    def _():
        pl.semaphore_signal(barrier, inc=1, device_id=above, device_id_type=MESH)

    @pl.when(has_down)
    def _():
        pl.semaphore_signal(barrier, inc=1, device_id=below, device_id_type=MESH)

    pl.semaphore_wait(barrier, n_row - 1 + has_up.astype(jnp.int32) + has_down.astype(jnp.int32))

    def part(ref, block, q):
        if ref is own_ref:
            return ref.at[block, pl.ds(pl.multiple_of(q * rows, 8), rows)]
        return ref.at[pl.ds(pl.multiple_of(block * rows_tile + q * rows, 8), rows)]

    def along_row(t, q, outward):
        peer = lax.rem(r + t, n_row)
        return pltpu.make_async_remote_copy(
            src_ref=part(own_ref, peer, q),
            dst_ref=part(out_ref, z * n_row + r if outward else z * n_row + lax.rem(r - t + n_row, n_row), q),
            send_sem=y_send.at[t * chunks + q],
            recv_sem=y_recv.at[t * chunks + q],
            device_id=(peer, c, z),
            device_id_type=MESH,
        )

    def along_rep(source, block, q, sems, target):
        return pltpu.make_async_remote_copy(
            src_ref=part(*source, q),
            dst_ref=part(out_ref, block, q),
            send_sem=sems.at[block * chunks + q],
            recv_sem=z_recv.at[block * chunks + q],
            device_id=target,
            device_id_type=MESH,
        )

    def forward(source, block, q):
        @pl.when(has_up)
        def _():
            along_rep(source, block, q, up_send, above).start()

        @pl.when(has_down)
        def _():
            along_rep(source, block, q, down_send, below).start()

    mine = z * n_row + r

    @pl.loop(0, chunks)
    def _(q):
        forward((own_ref, r), mine, q)
        for t in range(1, n_row):
            along_row(t, q, True).start()

    step = 16 if rows_tile % 16 == 0 else 8

    @pl.loop(0, rows_tile // step)
    def _(i):
        at = pl.ds(pl.multiple_of(i * step, step), step)
        to = pl.ds(pl.multiple_of(mine * rows_tile + i * step, step), step)
        out_ref[to, :] = own_ref[r, at, :]

    for t in range(1, n_row):

        @pl.loop(0, chunks)
        def _(q):
            along_row(t, q, False).wait_recv()
            block = z * n_row + lax.rem(r - t + n_row, n_row)
            forward((out_ref, block), block, q)

    def arrived(level, i, sems, target, onward):
        t, q = i // chunks, lax.rem(i, chunks)
        block = level * n_row + lax.rem(r - t + n_row, n_row)
        copy = along_rep((out_ref, block), block, q, sems, target)
        copy.wait_recv()

        @pl.when(onward)
        def _():
            copy.start()

    @pl.loop(1, n_rep)
    def _(d):
        @pl.loop(0, per_level)
        def _(i):
            @pl.when(z - d >= 0)
            def _():
                arrived(z - d, i, up_send, above, has_up)

            @pl.when(z + d < n_rep)
            def _():
                arrived(z + d, i, down_send, below, has_down)

    @pl.loop(0, chunks)
    def _(q):
        for t in range(1, n_row):
            along_row(t, q, True).wait_send()

    def drain(first, last, sems, target):
        @pl.loop(first * per_level, last * per_level)
        def _(i):
            block, q = i // chunks, lax.rem(i, chunks)
            along_rep((out_ref, block), block, q, sems, target).wait_send()

    @pl.when(has_up)
    def _():
        drain(0, z + 1, up_send, above)

    @pl.when(has_down)
    def _():
        drain(z, n_rep, down_send, below)


def gathered(own):
    n_row, n_rep = lax.axis_size("row"), lax.axis_size("rep")
    _, rows_tile, piece_cols = own.shape
    chunks = 4 if rows_tile % 64 == 0 else 1
    every = n_rep * n_row * chunks
    dma = pltpu.SemaphoreType.DMA
    return pl.pallas_call(
        functools.partial(gather_kernel, n_row, n_rep, chunks),
        out_shape=pltpu.VMEM((n_rep * n_row * rows_tile, piece_cols), own.dtype),
        in_specs=[pl.BlockSpec(memory_space=pltpu.VMEM)],
        out_specs=pl.BlockSpec(memory_space=pltpu.VMEM),
        scratch_shapes=[
            dma((n_row * chunks,)),
            dma((n_row * chunks,)),
            dma((every,)),
            dma((every,)),
            dma((every,)),
        ],
        compiler_params=pltpu.CompilerParams(
            collective_id=0, has_side_effects=True, vmem_limit_bytes=VMEM_LIMIT
        ),
    )(pltpu.with_memory_space_constraint(own, pltpu.VMEM))


def project_kernel(hidden_ref, landed_ref, served_ref, projected_ref, sem):
    parts = sem.shape[0]
    rows = served_ref.shape[0] // parts
    cols = served_ref.shape[1]
    copies = [
        pltpu.make_async_copy(
            landed_ref.at[pl.ds(i * rows, rows)], served_ref.at[pl.ds(i * rows, rows)], sem.at[i]
        )
        for i in range(parts)
    ]
    for copy in copies:
        copy.start()
    tile = 256 if cols % 256 == 0 else LANES

    @pl.loop(0, cols // tile)
    def _(n):
        at = pl.ds(pl.multiple_of(n * tile, tile), tile)
        projected_ref[:, at] = jnp.dot(
            hidden_ref[...], landed_ref[:, at], preferred_element_type=jnp.float32
        )

    for copy in copies:
        copy.wait()


def projected_and_stored(hidden, landed):
    rows, cols = landed.shape
    return pl.pallas_call(
        project_kernel,
        out_shape=(
            jax.ShapeDtypeStruct(landed.shape, landed.dtype),
            jax.ShapeDtypeStruct((hidden.shape[0], cols), jnp.float32),
        ),
        in_specs=[pl.BlockSpec(memory_space=pltpu.VMEM)] * 2,
        out_specs=(
            pl.BlockSpec(memory_space=pl.ANY),
            pl.BlockSpec(memory_space=pltpu.VMEM),
        ),
        scratch_shapes=[pltpu.SemaphoreType.DMA((8,))],
        compiler_params=pltpu.CompilerParams(vmem_limit_bytes=VMEM_LIMIT),
    )(hidden, pltpu.with_memory_space_constraint(landed, pltpu.VMEM))


def shards(hidden, train_weight, shard_order):
    landed = gathered(ordered_pieces(train_weight, shard_order))
    return projected_and_stored(hidden, landed)


def solution(mesh):
    placed = (P("rep", None), P(("rep", "row"), "col"), P())
    return jax.shard_map(
        shards,
        mesh=mesh,
        in_specs=placed,
        out_specs=(P(None, ("col", "row")), P("rep", ("col", "row"))),
        check_vma=False,
    )
```

time: 699 us -> 514 us (0.74)
  waiting for transfers between devices: 494 us -> 0 us
  Pallas kernels: 0 us -> 493 us
  blocking collectives: 92.8 us -> 0 us
  local copies, waits for them, and re-layouts: 65.1 us -> 20.4 us
  matrix products: 31.7 us -> 0 us
  between operations: 14.1 us -> 0.66 us
    all_gather x1 -> x0, waiting for transfers between devices: 494 us -> none  [shards(): served = lax.all_gather(column, 'rep', axis=0, tiled=True)]
    pallas_call x0 -> x3, Pallas kernels: none -> 493 us  [the longest x1 478 us: gathered(): pl.pallas_call(functools.partial(gather_kernel, n_row, n_rep, chunks), ou...]
    all_to_all x1 -> x0, blocking collectives: 92.8 us -> none  [shards(): lax.all_to_all(ordered, 'row', split_axis=1, concat_axis=0, tiled=True)]
    dot_general x2 -> x0, matrix products: 31.7 us -> none  [the longest x1 18.4 us: shards(): jnp.einsum('ksj,rjkc->rskc', selector, tiled, preferred_element_type=jnp....]
    convert_element_type x1 -> x0, local copies, waits for them, and re-layouts: 18.6 us -> none  [shards(): ordered = picked.astype(jnp.bfloat16).reshape(rows_tile, cols_tile)]
    reshape x1 -> x0, local copies, waits for them, and re-layouts: 12.8 us -> none  [shards(): tiled = train_weight.reshape(rows_tile, row_count, sub_count, sub_cols)]
    all_to_all x1 -> x0, local copies, waits for them, and re-layouts: 11.3 us -> none  [shards(): lax.all_to_all(ordered, 'row', split_axis=1, concat_axis=0, tiled=True)]
    unnamed x6 -> x7, local copies, waits for them, and re-layouts: 21.5 us -> 20.4 us
  transfers between devices with their start and end apart: 1 -> 0, of which waited for: 1 -> 0; matrix products, arithmetic and copies ran while one was open for 0% -> 0% of each run, Pallas kernels for 0% -> 0%
where the time goes in v1:
time: 514 us
  Pallas kernels  493 us (96%)
  local copies, waits for them, and re-layouts  20.4 us (4%)
    pallas_call x1, Pallas kernels, gathered(): pl.pallas_call(functools.partial(gather_kernel, n_row, n_rep, chunks), ou...  478 us
    unnamed x7, local copies, waits for them, and re-layouts  20.4 us
    pallas_call x1, Pallas kernels, projected_and_stored(): pl.pallas_call(project_kernel, out_shape=(jax.ShapeDtypeStruct(landed.sha...  10.8 us

profile of v1, /device:TPU:0, one launch (start us, length us, event | category | flops | bytes accessed | tf_op | source)
XLA Modules:
  0.0 513.8 jit_solution(15664370908669523281)
XLA Ops:
  0.6 0.8 copy.5.order_ref
  1.4 3.9 shard_map.50.own_ref
  5.3 0.0 copy-start.2
  5.3 478.0 %shard_map.51.landed_ref = bf16[7168,2048]{1,0:T(8,128)(2,1)S(1)} custom-call(bf16[2,896,2048]{2,1,0:T(8,128)(2,1)S(1)} %shard_map.50.own_ref), custom_call_target="tpu_custom_call" | custom-call | tf_op jit(solution)/shard_map/pallas_call | solution.py:195
  483.4 0.0 copy-start
  483.4 10.3 %copy-done = bf16[7168,2048]{1,0:T(8,128)(2,1)} copy-done((bf16[7168,2048]{1,0:T(8,128)(2,1)}, bf16[7168,2048]{1,0:T(8,128)(2,1)S(1)}, u32[]{:S(2)}) %copy-start) | copy-done | bytes 29360152
  493.7 0.0 copy-done.2
  493.7 0.0 copy-start.1
  493.7 9.3 %copy-done.1 = bf16[7168,2048]{1,0:T(8,128)(2,1)S(1)} copy-done((bf16[7168,2048]{1,0:T(8,128)(2,1)S(1)}, bf16[7168,2048]{1,0:T(8,128)(2,1)}, u32[]{:S(2)}) %copy-start.1) | copy-done | bytes 29360152
  503.0 10.8 %shard_map.52 = (bf16[7168,2048]{1,0:T(8,128)(2,1)}, f32[128,2048]{1,0:T(8,128)}) custom-call(bf16[128,7168]{1,0:T(8,128)(2,1)S(1)} %copy-done.2, bf16[7168,2048]{1,0:T(8,128)(2,1)S(1)} %copy-done.1), custom_call_target="tpu_custom_call" | custom-call | tf_op jit(solution)/shard_map/pallas_call | solution.py:240
Async XLA Ops:
  5.3 488.4 %copy-start.2 = (bf16[128,7168]{1,0:T(8,128)(2,1)S(1)}, bf16[128,7168]{1,0:T(8,128)(2,1)}, u32[]{:S(2)}) copy-start(bf16[128,7168]{1,0:T(8,128)(2,1)} %hidden_ref.1) | copy-start | bytes 5505028
  483.4 10.3 %copy-start = (bf16[7168,2048]{1,0:T(8,128)(2,1)}, bf16[7168,2048]{1,0:T(8,128)(2,1)S(1)}, u32[]{:S(2)}) copy-start(bf16[7168,2048]{1,0:T(8,128)(2,1)S(1)} %shard_map.51.landed_ref) | copy-start | bytes 88080384
  493.7 9.4 %copy-start.1 = (bf16[7168,2048]{1,0:T(8,128)(2,1)S(1)}, bf16[7168,2048]{1,0:T(8,128)(2,1)}, u32[]{:S(2)}) copy-start(bf16[7168,2048]{1,0:T(8,128)(2,1)} %copy-done) | copy-start | bytes 88080384

commit v2 on v1

--- a/solution.py
+++ b/solution.py
@@ -62,7 +62,7 @@
     return jnp.stack(pieces)
 
 
-def gather_kernel(n_row, n_rep, chunks, own_ref, out_ref, y_send, y_recv, z_recv, up_send, down_send):
+def gather_kernel(n_row, n_rep, chunks, own_ref, hidden_ref, out_ref, projected_ref, y_send, y_recv, z_recv, up_send, down_send):
     r, c, z = lax.axis_index("row"), lax.axis_index("col"), lax.axis_index("rep")
     rows_tile = own_ref.shape[1]
     rows = rows_tile // chunks
@@ -120,6 +120,26 @@
         def _():
             along_rep(source, block, q, down_send, below).start()
 
+    level_rows = n_row * rows_tile
+    by_level = level_rows % LANES == 0
+    cols = out_ref.shape[1]
+    tile = 256 if cols % 256 == 0 else LANES
+
+    def multiply(first, depth, fresh):
+        within = pl.ds(first, depth)
+
+        @pl.loop(0, cols // tile)
+        def _(n):
+            at = pl.ds(pl.multiple_of(n * tile, tile), tile)
+            term = jnp.dot(
+                hidden_ref[:, within], out_ref[within, at], preferred_element_type=jnp.float32
+            )
+            projected_ref[:, at] = term if fresh else projected_ref[:, at] + term
+
+    def add_level(level, fresh=False):
+        if by_level:
+            multiply(pl.multiple_of(level * level_rows, LANES), level_rows, fresh)
+
     mine = z * n_row + r
 
     @pl.loop(0, chunks)
@@ -153,6 +173,8 @@
         @pl.when(onward)
         def _():
             copy.start()
+
+    add_level(z, True)
 
     @pl.loop(1, n_rep)
     def _(d):
@@ -166,6 +188,17 @@
             def _():
                 arrived(z + d, i, down_send, below, has_down)
 
+        @pl.when(z - d >= 0)
+        def _():
+            add_level(z - d)
+
+        @pl.when(z + d < n_rep)
+        def _():
+            add_level(z + d)
+
+    if not by_level:
+        multiply(0, out_ref.shape[0], True)
+
     @pl.loop(0, chunks)
     def _(q):
         for t in range(1, n_row):
@@ -186,7 +219,7 @@
         drain(z, n_rep, down_send, below)
 
 
-def gathered(own):
+def gathered(own, hidden):
     n_row, n_rep = lax.axis_size("row"), lax.axis_size("rep")
     _, rows_tile, piece_cols = own.shape
     chunks = 4 if rows_tile % 64 == 0 else 1
@@ -194,9 +227,12 @@
     dma = pltpu.SemaphoreType.DMA
     return pl.pallas_call(
         functools.partial(gather_kernel, n_row, n_rep, chunks),
-        out_shape=pltpu.VMEM((n_rep * n_row * rows_tile, piece_cols), own.dtype),
-        in_specs=[pl.BlockSpec(memory_space=pltpu.VMEM)],
-        out_specs=pl.BlockSpec(memory_space=pltpu.VMEM),
+        out_shape=(
+            pltpu.VMEM((n_rep * n_row * rows_tile, piece_cols), own.dtype),
+            pltpu.VMEM((hidden.shape[0], piece_cols), jnp.float32),
+        ),
+        in_specs=[pl.BlockSpec(memory_space=pltpu.VMEM)] * 2,
+        out_specs=(pl.BlockSpec(memory_space=pltpu.VMEM),) * 2,
         scratch_shapes=[
             dma((n_row * chunks,)),
             dma((n_row * chunks,)),
@@ -207,13 +243,12 @@
         compiler_params=pltpu.CompilerParams(
             collective_id=0, has_side_effects=True, vmem_limit_bytes=VMEM_LIMIT
         ),
-    )(pltpu.with_memory_space_constraint(own, pltpu.VMEM))
-
-
-def project_kernel(hidden_ref, landed_ref, served_ref, projected_ref, sem):
+    )(pltpu.with_memory_space_constraint(own, pltpu.VMEM), hidden)
+
+
+def store_kernel(landed_ref, served_ref, sem):
     parts = sem.shape[0]
     rows = served_ref.shape[0] // parts
-    cols = served_ref.shape[1]
     copies = [
         pltpu.make_async_copy(
             landed_ref.at[pl.ds(i * rows, rows)], served_ref.at[pl.ds(i * rows, rows)], sem.at[i]
@@ -222,40 +257,24 @@
     ]
     for copy in copies:
         copy.start()
-    tile = 256 if cols % 256 == 0 else LANES
-
-    @pl.loop(0, cols // tile)
-    def _(n):
-        at = pl.ds(pl.multiple_of(n * tile, tile), tile)
-        projected_ref[:, at] = jnp.dot(
-            hidden_ref[...], landed_ref[:, at], preferred_element_type=jnp.float32
-        )
-
     for copy in copies:
         copy.wait()
 
 
-def projected_and_stored(hidden, landed):
-    rows, cols = landed.shape
+def stored(landed):
     return pl.pallas_call(
-        project_kernel,
-        out_shape=(
-            jax.ShapeDtypeStruct(landed.shape, landed.dtype),
-            jax.ShapeDtypeStruct((hidden.shape[0], cols), jnp.float32),
-        ),
-        in_specs=[pl.BlockSpec(memory_space=pltpu.VMEM)] * 2,
-        out_specs=(
-            pl.BlockSpec(memory_space=pl.ANY),
-            pl.BlockSpec(memory_space=pltpu.VMEM),
-        ),
+        store_kernel,
+        out_shape=jax.ShapeDtypeStruct(landed.shape, landed.dtype),
+        in_specs=[pl.BlockSpec(memory_space=pl.ANY)],
+        out_specs=pl.BlockSpec(memory_space=pl.ANY),
         scratch_shapes=[pltpu.SemaphoreType.DMA((8,))],
-        compiler_params=pltpu.CompilerParams(vmem_limit_bytes=VMEM_LIMIT),
-    )(hidden, pltpu.with_memory_space_constraint(landed, pltpu.VMEM))
+        compiler_params=pltpu.CompilerParams(vmem_limit_bytes=1024 * 1024),
+    )(landed)
 
 
 def shards(hidden, train_weight, shard_order):
-    landed = gathered(ordered_pieces(train_weight, shard_order))
-    return projected_and_stored(hidden, landed)
+    landed, projected = gathered(ordered_pieces(train_weight, shard_order), hidden)
+    return stored(landed), projected
 
 
 def solution(mesh):

time: 514 us -> 497 us (0.967)
  local copies, waits for them, and re-layouts: 20.4 us -> 1.77 us
    unnamed x7 -> x4, local copies, waits for them, and re-layouts: 20.4 us -> 1.77 us
where the time goes in v2:
time: 497 us
  Pallas kernels  494 us (99%)
    pallas_call x1, Pallas kernels, gathered(): pl.pallas_call(functools.partial(gather_kernel, n_row, n_rep, chunks), ou...  481 us

profile of v2, /device:TPU:0, one launch (start us, length us, event | category | flops | bytes accessed | tf_op | source)
XLA Modules:
  0.0 496.9 jit_solution(6754760068358220525)
XLA Ops:
  0.6 0.8 copy.5.order_ref
  1.4 0.0 copy-start
  1.4 3.9 shard_map.50.own_ref
  5.3 0.0 copy-done
  5.3 480.7 %shard_map.51 = (bf16[7168,2048]{1,0:T(8,128)(2,1)S(1)}, f32[128,2048]{1,0:T(8,128)S(1)}) custom-call(bf16[2,896,2048]{2,1,0:T(8,128)(2,1)S(1)} %shard_map.50.own_ref, bf16[128,7168]{1,0:T(8,128)(2,1)S(1)} %copy-done), custom_call_target="tpu_custom_call" | custom-call | tf_op jit(solution)/shard_map/pallas_call | solution.py:228
  486.1 9.8 %shard_map.52 = bf16[7168,2048]{1,0:T(8,128)(2,1)} custom-call(bf16[7168,2048]{1,0:T(8,128)(2,1)S(1)} %get-tuple-element.4.landed_ref), custom_call_target="tpu_custom_call" | custom-call | tf_op jit(solution)/shard_map/pallas_call | solution.py:265
  495.9 1.0 copy.7
Async XLA Ops:
  1.4 3.9 copy-start
